TPU v7x, 256 devices: a whole 4x4x8 slice. The times are simulated.
256 devices in a mesh: expert: 32 (over z_lo, y, core), tensor: 8 (over z_hi, x).
Axes of the slice: x: 4, y: 4, z: 8 (z_hi: 2, z_lo: 4; z = z_hi * 4 + z_lo), core: 2. Of those that a mesh axis runs over, the one named last changes fastest.
Arguments:
- tokens: bfloat16 [32768, 2048], P(('expert', 'tensor')), may hold values from -6 to 6
- assignment: int32 [32768], P(('expert', 'tensor')), may hold values from 0 to 31, as said below
- norm_gain: float32 [2048], replicated, may hold values from 0.25 to 1.75
- centroids: bfloat16 [32, 2048], replicated, may hold values from -0.125 to 0.125
- w_in: bfloat16 [32, 2048, 8192], P('expert', None, 'tensor'), may hold values from -0.125 to 0.125
- w_out: bfloat16 [32, 8192, 2048], P('expert', 'tensor'), may hold values from -0.0625 to 0.0625
Outputs:
- mixed: bfloat16 [32768, 2048], P(('expert', 'tensor'))
Inputs may be any that keep to these rules, and one draw needn't show every extreme that they name: `assignment`: in each device's block of 128 consecutive tokens every expert is named exactly 4 times.
All inputs are finite; a program needn't handle non-finite values.
Results may differ from a plain program's by a relative error of at most 0.006.
Values may be sent and summed in bfloat16 or wider, within the bound.
No kernel may reach another device: no remote copies, remote signals or barrier semaphores. Data moves between devices by JAX's collectives and lax.ppermute only.
A program may use at most 64 MiB of HBM per device.

v0:
```python
import jax
import jax.numpy as jnp
from jax import lax
from jax.sharding import Mesh
from jax.sharding import PartitionSpec as P

TENSOR = ("tensor_0", "tensor_1")
EXPERT_TENSOR = ("expert", "tensor_0", "tensor_1")


def reduced_to_own(blocks, axes, order):
    inside = blocks.shape[1:]
    blocks = blocks.reshape(*(lax.axis_size(a) for a in axes), *inside)
    blocks = jnp.moveaxis(blocks, order, range(len(axes))).reshape(-1, *inside)
    for k in order:
        blocks = lax.psum_scatter(blocks, axes[k], scatter_dimension=0, tiled=True)
    return blocks[0]


def split_up(shard, dim, size):
    lengths = shard.shape
    blocks = shard.reshape(*lengths[:dim], size, lengths[dim] // size, *lengths[dim + 1 :])
    return jnp.moveaxis(blocks, dim, 0)


def summed_rows(shard, axes, order, dim):
    size = lax.axis_size(axes)
    return reduced_to_own(split_up(shard, dim, size), axes, order)


def layer_norm(values, gain):
    widened = values.astype(jnp.float32)
    average = jnp.mean(widened, axis=1, keepdims=True)
    centred = widened - average
    variance = jnp.mean(centred * centred, axis=1, keepdims=True)
    return centred * lax.rsqrt(variance + 1e-05) * gain


def body(tokens, assignment, norm_gain, centroids, w_in, w_out):
    tok_rows = tokens.shape[0]
    num_experts = centroids.shape[0]
    per_expert = tok_rows // num_experts
    normed = layer_norm(tokens, norm_gain).astype(jnp.bfloat16)
    logits = jnp.dot(tokens, centroids.T, preferred_element_type=jnp.float32)
    column_ids = lax.broadcasted_iota(jnp.int32, (tok_rows, num_experts), 1)
    picked = jnp.sum(jnp.where(assignment[:, None] == column_ids, logits, 0.0), axis=1)
    gate_value = jax.nn.sigmoid(picked)
    same_expert = assignment[:, None] == assignment[None, :]
    row_ids = lax.broadcasted_iota(jnp.int32, (tok_rows, tok_rows), 0)
    col_ids = lax.broadcasted_iota(jnp.int32, (tok_rows, tok_rows), 1)
    rank_in = jnp.sum((same_expert & (col_ids < row_ids)).astype(jnp.int32), axis=1)
    slot_of = assignment * per_expert + rank_in
    ordering = jnp.argsort(slot_of)
    ordered_rows = normed[ordering]
    arrived = lax.all_to_all(ordered_rows, "expert", split_axis=0, concat_axis=0, tiled=True)
    w_first = w_in[0]
    w_second = w_out[0]
    hidden = jax.nn.gelu(
        jnp.dot(
            lax.all_gather(arrived, TENSOR, axis=0, tiled=True),
            w_first,
            preferred_element_type=jnp.float32,
        ),
        approximate=True,
    ).astype(jnp.bfloat16)
    partials = jnp.dot(hidden, w_second, preferred_element_type=jnp.float32).astype(jnp.bfloat16)
    summed = summed_rows(partials, TENSOR, (1, 0), 0).astype(jnp.float32).astype(jnp.bfloat16)
    returned = lax.all_to_all(summed, "expert", split_axis=0, concat_axis=0, tiled=True)
    expert_out = returned[slot_of]
    mixed = tokens.astype(jnp.float32) + gate_value[:, None] * expert_out.astype(jnp.float32)
    return mixed.astype(jnp.bfloat16)


def solution(mesh):
    finer = Mesh(
        mesh.devices.reshape(mesh.shape["expert"], 2, 4), ("expert", "tensor_0", "tensor_1")
    )
    return jax.shard_map(
        body,
        mesh=finer,
        in_specs=(
            P(EXPERT_TENSOR, None),
            P(EXPERT_TENSOR),
            P(),
            P(),
            P("expert", None, TENSOR),
            P("expert", TENSOR, None),
        ),
        out_specs=P(EXPERT_TENSOR, None),
        check_vma=False,
    )
```

profile of v0, /device:TPU:1, one launch (start us, length us, event | category | flops | bytes accessed | tf_op | source)
XLA Modules:
  0.0 288.4 jit_solution(13480588481350019458)
XLA Ops:
  6.5 1.2 convert_reduce_fusion
  7.8 1.3 fusion.23
  9.1 0.9 convert_reduce_fusion.1
  10.0 0.7 compare_select_fusion
  10.7 2.5 sort.17
  13.2 1.4 fusion.25
  14.7 0.9 gather_fusion
  15.6 0.2 all_to_all.16
  15.8 26.4 %all_to_all.24 = bf16[32,4,2048]{2,1,0:T(4,128)(2,1)S(1)} all-to-all(bf16[32,4,2048]{2,1,0:T(4,128)(2,1)S(1)} %all_to_all.16), channel_id=1, replica_groups=mesh['expert'=32,'tensor_0'=2,'tensor_1'=4] {'expert'}, dimensions={0} | all-to-all | bytes 1048576 | tf_op jit(solution)/shard_map/all_to_all | solution.py:55
  42.2 0.9 all_to_all.18
  43.2 0.0 reduce-scatter.3.cloned.1.call-start
  43.2 104.6 %all-gather.2.cloned.1.call-done = bf16[1024,2048]{1,0:T(8,128)(2,1)} async-done(((bf16[128,2048]{1,0:T(8,128)(2,1)}), bf16[1024,2048]{1,0:T(8,128)(2,1)}) %all-gather.2.cloned.1.call-update) | async-done | bytes 4194320 | tf_op jit(solution)/shard_map/all_gather | solution.py:60
  147.8 15.1 %fusion.12 = bf16[1024,2048]{1,0:T(8,128)(2,1)} fusion(bf16[1,1024,2048]{2,1,0:T(8,128)(2,1)} %param.11, bf16[1024,2048]{1,0:T(8,128)(2,1)} %all-gather.2.cloned.1.call-done, bf16[1,2048,1024]{2,1,0:T(8,128)(2,1)} %param.10), kind=kOutput, calls=%fused_computation.15 | convolution fusion | flops 8601468928 | bytes 16777216 | tf_op jit(solution)/shard_map/dot_general | solution.py:66
  163.0 4.7 %copy.8 = bf16[2,4,128,2048]{3,2,0,1:T(8,128)(2,1)} copy(bf16[2,4,128,2048]{3,2,1,0:T(8,128)(2,1)} %bitcast.20) | data formatting | bytes 8388608 | tf_op jit(solution)/shard_map/reshape;reshape | solution.py:13
  167.7 0.0 reduce-scatter.5.cloned.1.call-start
  167.8 44.8 %reduce-scatter.3.cloned.1.call-done = bf16[2,128,2048]{2,1,0:T(8,128)(2,1)} async-done(((bf16[8,128,2048]{2,1,0:T(8,128)(2,1)}), bf16[2,128,2048]{2,1,0:T(8,128)(2,1)}) %reduce-scatter.3.cloned.1.call-update) | async-done | bytes 1048592 | tf_op jit(solution)/shard_map/reduce_scatter | solution.py:16
  212.6 43.2 %reduce-scatter.5.cloned.1.call-done = bf16[1,128,2048]{2,1,0:T(8,128)(2,1)} async-done(((bf16[2,128,2048]{2,1,0:T(8,128)(2,1)}), bf16[1,128,2048]{2,1,0:T(8,128)(2,1)}) %reduce-scatter.5.cloned.1.call-update) | async-done | bytes 524304 | tf_op jit(solution)/shard_map/reduce_scatter | solution.py:16
  255.8 2.0 all_to_all.19
  257.8 5.5 %all-to-all-start.1 = ((bf16[32,4,2048]{2,1,0:T(4,128)(2,1)}), bf16[32,4,2048]{2,1,0:T(4,128)(2,1)S(1)}, u32[]{:S(2)}, u32[]{:S(2)}) async-start(bf16[32,4,2048]{2,1,0:T(4,128)(2,1)} %all_to_all.19), calls=%async_computation.3 | async-start | bytes 1048576 | tf_op jit(solution)/shard_map/all_to_all | solution.py:68
  263.4 0.3 fusion.22
  263.7 16.1 %all-to-all-done.1 = bf16[32,4,2048]{2,1,0:T(4,128)(2,1)S(1)} async-done(((bf16[32,4,2048]{2,1,0:T(4,128)(2,1)}), bf16[32,4,2048]{2,1,0:T(4,128)(2,1)S(1)}, u32[]{:S(2)}, u32[]{:S(2)}) %all-to-all-start.1) | async-done | bytes 524320 | tf_op jit(solution)/shard_map/all_to_all | solution.py:68
  279.7 0.1 all_to_all.21
  279.9 0.9 gather_fusion.1
  280.8 1.0 fusion.26
  (17 shorter events, 0.1 us)
Async XLA Ops:
  6.5 256.8 %copy-start = (bf16[32,2048]{1,0:T(8,128)(2,1)S(1)}, bf16[32,2048]{1,0:T(8,128)(2,1)}, u32[]{:S(2)}) copy-start(bf16[32,2048]{1,0:T(8,128)(2,1)} %param.9) | copy-start | bytes 393220
  6.5 141.3 %all-gather.2.cloned.1.call-start = ((), (), s32[]{:S(2)}) async-start(), calls=%async_computation.4 | async-start | bytes 4718592 | tf_op jit(solution)/shard_map/all_gather | solution.py:60
  43.2 169.4 %reduce-scatter.3.cloned.1.call-start = ((), (), s32[]{:S(2)}) async-start(), calls=%async_computation.5 | async-start | bytes 5242880 | tf_op jit(solution)/shard_map/reduce_scatter | solution.py:16
  167.7 95.6 %copy-start.1 = (bf16[128,2048]{1,0:T(8,128)(2,1)S(1)}, bf16[128,2048]{1,0:T(8,128)(2,1)}, u32[]{:S(2)}) copy-start(bf16[128,2048]{1,0:T(8,128)(2,1)} %param.6) | copy-start | bytes 1572868
  167.7 95.6 %copy-start.2 = (s32[128]{0:T(128)S(1)}, s32[128]{0:T(128)}, u32[]{:S(2)}) copy-start(s32[128]{0:T(128)} %param.7) | copy-start | bytes 1540
  167.7 88.1 %reduce-scatter.5.cloned.1.call-start = ((), (), s32[]{:S(2)}) async-start(), calls=%async_computation.6 | async-start | bytes 1572864 | tf_op jit(solution)/shard_map/reduce_scatter | solution.py:16
  257.8 21.9 %all-to-all-start.1 = ((bf16[32,4,2048]{2,1,0:T(4,128)(2,1)}), bf16[32,4,2048]{2,1,0:T(4,128)(2,1)S(1)}, u32[]{:S(2)}, u32[]{:S(2)}) async-start(bf16[32,4,2048]{2,1,0:T(4,128)(2,1)} %all_to_all.19), calls=%async_computation.3 | async-start | bytes 1048576 | tf_op jit(solution)/shard_map/all_to_all | solution.py:68
Sparse Core Ops, SparseCore 0:
  43.3 104.5 all-gather.1
  167.9 44.6 reduce-scatter.2
  215.0 40.6 reduce-scatter.4
where the time goes:
time: 289 us; the launch traced here: 288 us
  waiting for transfers between devices  209 us (72%)
  blocking collectives  26.4 us (9%)
  matrix products  15.4 us (5%)
  between operations  13.2 us (5%)
  local copies, waits for them, and re-layouts  9.88 us (3%)
  other arithmetic  9.13 us (3%)
  starting transfers between devices  5.57 us (2%)
    all_gather x1, waiting for transfers between devices, body(): lax.all_gather(arrived, TENSOR, axis=0, tiled=True)  105 us
    reduce_scatter x2, waiting for transfers between devices, reduced_to_own(): blocks = lax.psum_scatter(blocks, axes[k], scatter_dimension=0, tiled=True)  88 us
    all_to_all x1, blocking collectives, body(): lax.all_to_all(ordered_rows, 'expert', split_axis=0, concat_axis=0, tiled...  26.4 us
    all_to_all x1, waiting for transfers between devices, body(): lax.all_to_all(summed, 'expert', split_axis=0, concat_axis=0, tiled=True)  16.1 us
    dot_general x1, matrix products, body(): jnp.dot(hidden, w_second, preferred_element_type=jnp.float32)  15.1 us
  transfers between devices with their start and end apart: 4, of which 4 were waited for; matrix products, arithmetic and copies ran while one was open for 0% of the time, Pallas kernels for 0%

commit v1 on v0

--- a/solution.py
+++ b/solution.py
@@ -6,6 +6,13 @@
 
 TENSOR = ("tensor_0", "tensor_1")
 EXPERT_TENSOR = ("expert", "tensor_0", "tensor_1")
+
+
+def exchange_gather(array, name, dim):
+    n_dev = lax.axis_size(name)
+    blocks = jnp.stack([array for _ in range(n_dev)])
+    blocks = lax.all_to_all(blocks, name, split_axis=0, concat_axis=0)
+    return jnp.concatenate(blocks, axis=dim)
 
 
 def reduced_to_own(blocks, axes, order):
@@ -56,11 +63,7 @@
     w_first = w_in[0]
     w_second = w_out[0]
     hidden = jax.nn.gelu(
-        jnp.dot(
-            lax.all_gather(arrived, TENSOR, axis=0, tiled=True),
-            w_first,
-            preferred_element_type=jnp.float32,
-        ),
+        jnp.dot(exchange_gather(arrived, TENSOR, 0), w_first, preferred_element_type=jnp.float32),
         approximate=True,
     ).astype(jnp.bfloat16)
     partials = jnp.dot(hidden, w_second, preferred_element_type=jnp.float32).astype(jnp.bfloat16)

time: 289 us -> 289 us (level)
  waiting for transfers between devices: 209 us -> 115 us
  blocking collectives: 26.4 us -> 120 us
    all_gather x1 -> x0, waiting for transfers between devices: 105 us -> none  [body(): lax.all_gather(arrived, TENSOR, axis=0, tiled=True)]
    all_to_all x0 -> x1, blocking collectives: none -> 93.4 us  [exchange_gather(): blocks = lax.all_to_all(blocks, name, split_axis=0, concat_axis=0)]
    reduce_scatter x2, waiting for transfers between devices: 88 us -> 99 us  [reduced_to_own(): blocks = lax.psum_scatter(blocks, axes[k], scatter_dimension=0, tiled=True)]
  transfers between devices with their start and end apart: 4 -> 3, of which waited for: 4 -> 3; matrix products, arithmetic and copies ran while one was open for 0% -> 0% of each run, Pallas kernels for 0% -> 0%
where the time goes in v1:
time: 289 us; the launch traced here: 288 us
  blocking collectives  120 us (42%)
  waiting for transfers between devices  115 us (40%)
  matrix products  15.4 us (5%)
  between operations  13.5 us (5%)
  local copies, waits for them, and re-layouts  9.61 us (3%)
  other arithmetic  9.13 us (3%)
  starting transfers between devices  5.49 us (2%)
    reduce_scatter x2, waiting for transfers between devices, reduced_to_own(): blocks = lax.psum_scatter(blocks, axes[k], scatter_dimension=0, tiled=True)  99 us
    all_to_all x1, blocking collectives, exchange_gather(): blocks = lax.all_to_all(blocks, name, split_axis=0, concat_axis=0)  93.4 us
    all_to_all x1, blocking collectives, body(): lax.all_to_all(ordered_rows, 'expert', split_axis=0, concat_axis=0, tiled...  26.4 us
    all_to_all x1, waiting for transfers between devices, body(): lax.all_to_all(summed, 'expert', split_axis=0, concat_axis=0, tiled=True)  16.1 us
    dot_general x1, matrix products, body(): jnp.dot(hidden, w_second, preferred_element_type=jnp.float32)  15.1 us
  transfers between devices with their start and end apart: 3, of which 3 were waited for; matrix products, arithmetic and copies ran while one was open for 0% of the time, Pallas kernels for 0%

profile of v1, /device:TPU:1, one launch (start us, length us, event | category | flops | bytes accessed | tf_op | source)
XLA Modules:
  0.0 288.1 jit_solution(9070889836561830212)
XLA Ops:
  6.5 1.2 convert_reduce_fusion
  7.8 1.3 fusion.23
  9.1 0.9 convert_reduce_fusion.1
  10.0 0.7 compare_select_fusion
  10.7 2.5 sort.17
  13.2 1.4 fusion.25
  14.7 0.9 gather_fusion
  15.6 0.2 all_to_all.17
  15.8 26.4 %all_to_all.26 = bf16[32,4,2048]{2,1,0:T(4,128)(2,1)S(1)} all-to-all(bf16[32,4,2048]{2,1,0:T(4,128)(2,1)S(1)} %all_to_all.17), channel_id=1, replica_groups=mesh['expert'=32,'tensor_0'=2,'tensor_1'=4] {'expert'}, dimensions={0} | all-to-all | bytes 1048576 | tf_op jit(solution)/shard_map/all_to_all | solution.py:62
  42.2 0.1 stack.4
  42.3 0.5 stack.5
  42.9 93.4 %all_to_all.27 = bf16[8,128,2048]{2,1,0:T(8,128)(2,1)} all-to-all(bf16[8,128,2048]{2,1,0:T(8,128)(2,1)S(1)} %stack.5), channel_id=1, replica_groups=mesh['expert'=32,'tensor_0'=2,'tensor_1'=4] {'tensor_0','tensor_1'}, dimensions={0} | all-to-all | bytes 8388608 | tf_op jit(solution)/shard_map/all_to_all | solution.py:14
  136.2 15.1 %fusion.12 = bf16[1024,2048]{1,0:T(8,128)(2,1)} fusion(bf16[1,1024,2048]{2,1,0:T(8,128)(2,1)} %param.11, bf16[1024,2048]{1,0:T(8,128)(2,1)} %bitcast.21, bf16[1,2048,1024]{2,1,0:T(8,128)(2,1)} %param.10), kind=kOutput, calls=%fused_computation.15 | convolution fusion | flops 8601468928 | bytes 16777216 | tf_op jit(solution)/shard_map/dot_general | solution.py:69
  151.4 4.7 %copy.8 = bf16[2,4,128,2048]{3,2,0,1:T(8,128)(2,1)} copy(bf16[2,4,128,2048]{3,2,1,0:T(8,128)(2,1)} %bitcast.22) | data formatting | bytes 8388608 | tf_op jit(solution)/shard_map/reshape;reshape | solution.py:20
  156.1 0.0 reduce-scatter.5.cloned.1.call-start
  156.2 55.8 %reduce-scatter.3.cloned.1.call-done = bf16[2,128,2048]{2,1,0:T(8,128)(2,1)} async-done(((bf16[8,128,2048]{2,1,0:T(8,128)(2,1)}), bf16[2,128,2048]{2,1,0:T(8,128)(2,1)}) %reduce-scatter.3.cloned.1.call-update) | async-done | bytes 1048592 | tf_op jit(solution)/shard_map/reduce_scatter | solution.py:23
  212.0 43.2 %reduce-scatter.5.cloned.1.call-done = bf16[1,128,2048]{2,1,0:T(8,128)(2,1)} async-done(((bf16[2,128,2048]{2,1,0:T(8,128)(2,1)}), bf16[1,128,2048]{2,1,0:T(8,128)(2,1)}) %reduce-scatter.5.cloned.1.call-update) | async-done | bytes 524304 | tf_op jit(solution)/shard_map/reduce_scatter | solution.py:23
  255.2 2.0 all_to_all.20
  257.3 5.4 %all-to-all-start.2 = ((bf16[32,4,2048]{2,1,0:T(4,128)(2,1)}), bf16[32,4,2048]{2,1,0:T(4,128)(2,1)S(1)}, u32[]{:S(2)}, u32[]{:S(2)}) async-start(bf16[32,4,2048]{2,1,0:T(4,128)(2,1)} %all_to_all.20), calls=%async_computation.4 | async-start | bytes 1048576 | tf_op jit(solution)/shard_map/all_to_all | solution.py:71
  262.8 0.3 fusion.22
  263.1 16.1 %all-to-all-done.2 = bf16[32,4,2048]{2,1,0:T(4,128)(2,1)S(1)} async-done(((bf16[32,4,2048]{2,1,0:T(4,128)(2,1)}), bf16[32,4,2048]{2,1,0:T(4,128)(2,1)S(1)}, u32[]{:S(2)}, u32[]{:S(2)}) %all-to-all-start.2) | async-done | bytes 524320 | tf_op jit(solution)/shard_map/all_to_all | solution.py:71
  279.2 0.1 all_to_all.22
  279.3 0.9 gather_fusion.1
  280.2 1.0 fusion.26
  (16 shorter events, 0.1 us)
Async XLA Ops:
  6.5 256.2 %copy-start = (bf16[32,2048]{1,0:T(8,128)(2,1)S(1)}, bf16[32,2048]{1,0:T(8,128)(2,1)}, u32[]{:S(2)}) copy-start(bf16[32,2048]{1,0:T(8,128)(2,1)} %param.9) | copy-start | bytes 393220
  6.5 205.5 %reduce-scatter.3.cloned.1.call-start = ((), (), s32[]{:S(2)}) async-start(), calls=%async_computation.5 | async-start | bytes 5242880 | tf_op jit(solution)/shard_map/reduce_scatter | solution.py:23
  156.1 106.6 %copy-start.1 = (bf16[128,2048]{1,0:T(8,128)(2,1)S(1)}, bf16[128,2048]{1,0:T(8,128)(2,1)}, u32[]{:S(2)}) copy-start(bf16[128,2048]{1,0:T(8,128)(2,1)} %param.6) | copy-start | bytes 1572868
  156.1 106.6 %copy-start.2 = (s32[128]{0:T(128)S(1)}, s32[128]{0:T(128)}, u32[]{:S(2)}) copy-start(s32[128]{0:T(128)} %param.7) | copy-start | bytes 1540
  156.1 99.1 %reduce-scatter.5.cloned.1.call-start = ((), (), s32[]{:S(2)}) async-start(), calls=%async_computation.6 | async-start | bytes 1572864 | tf_op jit(solution)/shard_map/reduce_scatter | solution.py:23
  257.3 21.9 %all-to-all-start.2 = ((bf16[32,4,2048]{2,1,0:T(4,128)(2,1)}), bf16[32,4,2048]{2,1,0:T(4,128)(2,1)S(1)}, u32[]{:S(2)}, u32[]{:S(2)}) async-start(bf16[32,4,2048]{2,1,0:T(4,128)(2,1)} %all_to_all.20), calls=%async_computation.4 | async-start | bytes 1048576 | tf_op jit(solution)/shard_map/all_to_all | solution.py:71
Sparse Core Ops, SparseCore 0:
  156.3 55.7 reduce-scatter.2
  214.5 40.6 reduce-scatter.4
